TPU v7x, 32 devices: a whole 2x2x4 slice. The times are simulated.
32 devices in a mesh: groups: 2 (over y), graph: 16 (over z, x, core).
Axes of the slice: x: 2, y: 2, z: 4, core: 2. Of those that a mesh axis runs over, the one named last changes fastest.
Arguments:
- edge_state: bfloat16 [8192, 512], P(('groups', 'graph')), parts along dimension 0, may hold values from -6 to 6
- atom_state: bfloat16 [512, 256], P(('groups', 'graph')), parts along dimension 0, may hold values from -6 to 6
- atom_sends: int32 [4096], P(('groups', 'graph')), parts along dimension 0, may hold values from 0 to 15
- edge_source: int32 [8192], P(('groups', 'graph')), parts along dimension 0, may hold values from 0 to 127
- edge_target: int32 [8192], P(('groups', 'graph')), parts along dimension 0, may hold values from 0 to 15
- send_edges: int32 [262144], P(('groups', 'graph')), parts along dimension 0, may hold values from 0 to 255
- triplet_in: int32 [262144], P(('groups', 'graph')), parts along dimension 0, may hold values from 0 to 8191, as said below
- triplet_out: int32 [262144], P(('groups', 'graph')), parts along dimension 0, may hold values from 0 to 8191, as said below
- triplet_valid: int32 [262144], P(('groups', 'graph')), parts along dimension 0, may hold values 0 or 1
- triplet_basis: bfloat16 [16, 262144], P(None, ('groups', 'graph')), parts along dimension 1, may hold values from -6 to 6
- return_edges: int32 [262144], P(('groups', 'graph')), parts along dimension 0, may hold values from 0 to 255
- w_edge: bfloat16 [512, 512], replicated, may hold values from -0.25 to 0.25
- w_source: bfloat16 [256, 512], replicated, may hold values from -0.375 to 0.375
- w_down: bfloat16 [512, 64], replicated, may hold values from -0.25 to 0.25
- w_bilinear: bfloat16 [64, 1024], replicated, may hold values from -0.1875 to 0.1875
- w_up: bfloat16 [64, 512], replicated, may hold values from -0.125 to 0.125
- w_residual: bfloat16 [4, 512, 512], replicated, may hold values from -0.25 to 0.25
- w_atom: bfloat16 [512, 256], replicated, may hold values from -0.25 to 0.25
Outputs:
- edge_out: bfloat16 [8192, 512], P(('groups', 'graph')), parts along dimension 0
- atom_out: bfloat16 [512, 256], P(('groups', 'graph')), parts along dimension 0
There are 2 independent parts, one for each index of `groups`. A program takes and returns all parts, laid end to end along the dimension named above; an argument that names none is the same for every part. Nothing has to cross between parts.
Inputs may be any that keep to these rules, and one draw needn't show every extreme that they name: `atom_sends`: entry d * 8 + c of a device's 128 entries is sent to device d. `send_edges`: entry t * 512 + c of a device's 8192 entries is sent to tile t. `triplet_in`: triplet j of a tile reads a received slot in the same aligned block of 512 slots as j. `triplet_out`: slot d * 512 + c of a tile is returned to device d; triplet j of a tile adds to a slot in the same aligned block of 512 slots as j. `return_edges`: entry t * 512 + c of a device's 8192 entries belongs to the slot that tile t returns in place c.
All inputs are finite; a program needn't handle non-finite values. No bound on the sum of `triplet_valid` on one device may be relied on, other than what follows from the above.
Results may differ from a plain program's by a relative error of at most 0.0095.
Values may be sent and summed in bfloat16 or wider, within the bound.
A program may use at most 64 MiB of HBM per device.

v0:
```python
import functools

import jax
import jax.numpy as jnp
from jax import lax
from jax.experimental import pallas as pl
from jax.experimental.pallas import tpu as pltpu
from jax.sharding import PartitionSpec as P

WIN = 512


inv_root = 0.7071067811865476


def matmul(left, right):
    return jnp.dot(left, right, preferred_element_type=jnp.float32)


def pick_rows(indices, table):
    chooser = (indices[:, None] == jnp.arange(table.shape[0], dtype=jnp.int32)[None, :]).astype(
        table.dtype
    )
    return matmul(chooser, table).astype(table.dtype)


def bilinear_terms(inputs_x, coeffs, keeps, w_bilinear):
    expanded = matmul(inputs_x, w_bilinear)
    expanded = expanded.reshape(inputs_x.shape[0], coeffs.shape[0], -1)
    mixed = jnp.einsum("tkd,kt->td", expanded, coeffs.astype(jnp.float32))
    return mixed * keeps.astype(jnp.float32)[:, None]


def tile_sums(slot_rows, local_in, local_out, keeps, coeffs, w_bilinear):
    trip_count = slot_rows.shape[0]
    block_size = WIN
    block_count = trip_count // block_size
    basis_rows = coeffs.shape[0]
    block_iota = jnp.arange(block_size, dtype=jnp.int32)

    def one_block(operands):
        rows_blk, in_blk, out_blk, keep_blk, coef_blk = operands
        in_hot = ((in_blk % block_size)[:, None] == block_iota[None, :]).astype(jnp.bfloat16)
        inputs_x = matmul(in_hot, rows_blk).astype(jnp.bfloat16)
        mixed = bilinear_terms(inputs_x, coef_blk, keep_blk, w_bilinear)
        out_hot = (block_iota[:, None] == (out_blk % block_size)[None, :]).astype(jnp.float32)
        return jnp.dot(
            out_hot, mixed, precision=lax.Precision.HIGHEST, preferred_element_type=jnp.float32
        )

    shaped_coeffs = jnp.transpose(coeffs.reshape(basis_rows, block_count, block_size), (1, 0, 2))
    summed = lax.map(
        one_block,
        (
            slot_rows.reshape(block_count, block_size, -1),
            local_in.reshape(block_count, block_size),
            local_out.reshape(block_count, block_size),
            keeps.reshape(block_count, block_size),
            shaped_coeffs,
        ),
    )
    return summed.reshape(trip_count, -1).astype(jnp.bfloat16)


def plain_on_device(
    edge_state,
    atom_state,
    atom_sends,
    edge_source,
    edge_target,
    send_edges,
    triplet_in,
    triplet_out,
    triplet_valid,
    triplet_basis,
    return_edges,
    w_edge,
    w_source,
    w_down,
    w_bilinear,
    w_up,
    w_residual,
    w_atom,
):
    edge_count = edge_state.shape[0]
    atom_count = atom_state.shape[0]
    arrived_atoms = lax.all_to_all(
        pick_rows(atom_sends, atom_state), "graph", split_axis=0, concat_axis=0, tiled=True
    )
    src_rows = pick_rows(edge_source, arrived_atoms)
    pre_act = matmul(edge_state, w_edge) + matmul(src_rows, w_source)
    activated = jax.nn.silu(pre_act).astype(jnp.bfloat16)
    projected = jax.nn.silu(matmul(activated, w_down)).astype(jnp.bfloat16)
    slot_rows = lax.all_to_all(
        pick_rows(send_edges, projected), "graph", split_axis=0, concat_axis=0, tiled=True
    )
    slot_sums = tile_sums(
        slot_rows, triplet_in, triplet_out, triplet_valid, triplet_basis, w_bilinear
    )
    returned = lax.all_to_all(slot_sums, "graph", split_axis=0, concat_axis=0, tiled=True)
    back_hot = (jnp.arange(edge_count, dtype=jnp.int32)[:, None] == return_edges[None, :]).astype(
        jnp.bfloat16
    )
    aggregate = matmul(back_hot, returned)
    update = jax.nn.silu(matmul(aggregate.astype(jnp.bfloat16), w_up))
    base = ((edge_state.astype(jnp.float32) + activated.astype(jnp.float32)) * inv_root).astype(
        jnp.bfloat16
    )
    inner_one = jax.nn.silu(matmul(base, w_residual[0])).astype(jnp.bfloat16)
    middle = (
        (base.astype(jnp.float32) + jax.nn.silu(matmul(inner_one, w_residual[1]))) * inv_root
    ).astype(jnp.bfloat16)
    inner_two = jax.nn.silu(matmul(middle, w_residual[2])).astype(jnp.bfloat16)
    chain = (middle.astype(jnp.float32) + jax.nn.silu(matmul(inner_two, w_residual[3]))) * inv_root
    edge_out = (chain + update).astype(jnp.bfloat16)
    contrib = matmul(edge_out, w_atom).astype(jnp.bfloat16)
    one_hot = (edge_target[None, :] == jnp.arange(atom_count, dtype=jnp.int32)[:, None]).astype(
        jnp.bfloat16
    )
    atom_sum = matmul(one_hot, contrib)
    atom_out = (atom_state.astype(jnp.float32) + jax.nn.silu(0.25 * atom_sum)).astype(jnp.bfloat16)
    return (edge_out, atom_out)


def silu(value):
    return value / (1.0 + jnp.exp(-value))


def dot_at(left, right, left_dim, right_dim):
    return lax.dot_general(
        left, right, (((left_dim,), (right_dim,)), ((), ())), preferred_element_type=jnp.float32
    )


def hot_columns(row_count, indices):
    rows = lax.broadcasted_iota(jnp.int32, (row_count, indices.shape[1]), 0)
    return jnp.where(rows == indices, 1.0, 0.0).astype(jnp.bfloat16)


def partner(me, step, n):
    peer = me
    bit = 1
    while bit < n:
        mine = lax.rem(lax.div(me, bit), 2)
        flip = (step // bit) % 2 if isinstance(step, int) else lax.rem(lax.div(step, bit), 2)
        peer = peer + flip * (1 - 2 * mine) * bit
        bit *= 2
    return peer


def look_up(table, indices):
    lanes = 128
    found = []
    for start in range(0, indices.shape[1], lanes):
        wanted = jnp.broadcast_to(indices[:, start : start + lanes], (8, lanes))
        lane = wanted & (lanes - 1)
        value = jnp.zeros_like(wanted)
        for first in range(0, table.shape[1], lanes):
            part = jnp.take_along_axis(
                jnp.broadcast_to(table[:, first : first + lanes], (8, lanes)),
                lane,
                axis=1,
                mode="promise_in_bounds",
            )
            value = jnp.where(wanted - lane == first, part, value)
        found.append(value)
    return jnp.concatenate(found, axis=1)


def hot_from(row_count, eight_rows):
    rows = lax.broadcasted_iota(jnp.int32, (row_count, eight_rows.shape[1]), 0)
    spread = jnp.concatenate([eight_rows] * (row_count // 8), axis=0)
    return jnp.where(rows == spread, 1.0, 0.0).astype(jnp.bfloat16)


def tail_kernel(sum_v, chain_v, atom_v, target_v, w_up_v, w_atom_v, edge_out_ref, atom_out_ref):
    aggregate = sum_v[...].T.astype(jnp.bfloat16)
    update = silu(matmul(aggregate, w_up_v[...]))
    edge_out = (chain_v[...] + update).astype(jnp.bfloat16)
    edge_out_ref[...] = edge_out
    contrib = matmul(edge_out, w_atom_v[...]).astype(jnp.bfloat16)
    atom_sum = matmul(hot_columns(atom_v.shape[0], target_v[...]), contrib)
    atom_out_ref[...] = (atom_v[...].astype(jnp.float32) + silu(0.25 * atom_sum)).astype(
        jnp.bfloat16
    )


def block_kernel(n, loaded, *refs):
    sources = refs[:loaded]
    in_hbm, out_hbm, valid_hbm, basis_hbm = refs[loaded : loaded + 4]
    chain_v, sum_v = refs[loaded + 4 : loaded + 6]
    held = refs[loaded + 6 : 2 * loaded + 6]
    (
        stage_v,
        ends_v,
        stage_basis_v,
        basis_v,
        atoms_out,
        atoms_in,
        table_v,
        expand_v,
        load_sem,
        stage_sem,
        send_sem,
        recv_sem,
    ) = refs[2 * loaded + 6 :]
    (
        atom_v,
        asend_v,
        edge_v,
        w_edge_v,
        source_v,
        w_source_v,
        w_down_v,
        w_bilinear_v,
        w_res_v,
        send_v,
        return_v,
    ) = held
    me = lax.axis_index("graph")
    cap = ends_v.shape[3]
    edge_count = edge_v.shape[0]
    width = w_down_v.shape[0]
    basis_count = basis_v.shape[1]

    barrier = pltpu.get_barrier_semaphore()
    for step in range(1, n):
        pl.semaphore_signal(
            barrier,
            inc=1,
            device_id={"graph": partner(me, step, n)},
            device_id_type=pl.DeviceIdType.MESH,
        )
    loads = [
        pltpu.make_async_copy(src, dst, load_sem.at[i])
        for i, (src, dst) in enumerate(zip(sources, held))
    ]
    for load in loads:
        load.start()
    stages = [
        pltpu.make_async_copy(src, stage_v.at[:, i], stage_sem.at[i])
        for i, src in enumerate((in_hbm, out_hbm, valid_hbm))
    ]
    stages.append(pltpu.make_async_copy(basis_hbm, stage_basis_v, stage_sem.at[3]))
    for stage in stages:
        stage.start()
    loads[0].wait()
    loads[1].wait()
    picked = dot_at(hot_columns(atom_v.shape[0], asend_v[...]), atom_v[...], 0, 0)
    atoms_out[...] = picked.reshape(atoms_out.shape).astype(jnp.bfloat16)
    pl.semaphore_wait(barrier, n - 1)

    def parts(peer):
        lanes = pl.ds(pl.multiple_of(peer * cap, cap), cap)
        return (
            (atoms_out.at[peer], atoms_in.at[me]),
            (stage_v.at[peer], ends_v.at[me]),
            (stage_basis_v.at[:, lanes], basis_v.at[me]),
        )

    sent = []
    for kinds in ((0,), (1, 2)):
        if kinds[0]:
            for stage in stages:
                stage.wait()
        for step in range(n):
            peer = partner(me, step, n)
            for kind in kinds:
                src, dst = parts(peer)[kind]
                if step == 0:
                    copy = pltpu.make_async_copy(src, dst, recv_sem.at[kind, step])
                else:
                    copy = pltpu.make_async_remote_copy(
                        src_ref=src,
                        dst_ref=dst,
                        send_sem=send_sem.at[kind, step],
                        recv_sem=recv_sem.at[kind, step],
                        device_id={"graph": peer},
                        device_id_type=pl.DeviceIdType.MESH,
                    )
                    sent.append(copy)
                copy.start()

    def arrive(kind, buffer, step, peer):
        pltpu.make_async_copy(buffer.at[peer], buffer.at[peer], recv_sem.at[kind, step]).wait()

    for load in loads[2:7]:
        load.wait()
    edge = edge_v[...]
    pre_act = matmul(edge, w_edge_v[...])
    pick = hot_columns(atoms_in.shape[0] * atoms_in.shape[1], source_v[...])
    for step in range(n):
        arrive(0, atoms_in, step, partner(me, step, n))
    arrived = atoms_in[...].astype(jnp.float32).reshape(pick.shape[0], -1).astype(jnp.bfloat16)
    src_rows = dot_at(pick, arrived, 0, 0).astype(jnp.bfloat16)
    activated = silu(pre_act + matmul(src_rows, w_source_v[...])).astype(jnp.bfloat16)
    projected = silu(dot_at(activated, w_down_v[...], 1, 1)).astype(jnp.bfloat16)
    for load in loads[7:]:
        load.wait()
    table_v[...] = dot_at(w_bilinear_v[...], projected, 0, 1).astype(jnp.bfloat16)
    base = ((edge.astype(jnp.float32) + activated.astype(jnp.float32)) * inv_root).astype(
        jnp.bfloat16
    )
    inner_one = silu(matmul(base, w_res_v[0])).astype(jnp.bfloat16)
    middle = ((base.astype(jnp.float32) + silu(matmul(inner_one, w_res_v[1]))) * inv_root).astype(
        jnp.bfloat16
    )
    inner_two = silu(matmul(middle, w_res_v[2])).astype(jnp.bfloat16)
    chain_v[...] = (middle.astype(jnp.float32) + silu(matmul(inner_two, w_res_v[3]))) * inv_root
    sum_v[...] = jnp.zeros_like(sum_v)

    def some_tiles(group, carry):
        tiles = []
        for slot in range(expand_v.shape[0]):
            step = group * expand_v.shape[0] + slot
            tile = partner(me, step, n)
            tiles.append(tile)
            arrive(1, ends_v, step, tile)
            arrive(2, basis_v, step, tile)
        for slot, tile in enumerate(tiles):
            in_hot = hot_from(edge_count, look_up(send_v[tile], ends_v[tile, 0] & (cap - 1)))
            expand_v[slot] = matmul(table_v[...], in_hot)
            coeffs = basis_v[tile].astype(jnp.float32) * ends_v[tile, 2].astype(jnp.float32)
            mixed = jnp.zeros((width, cap), jnp.float32)
            for k in range(basis_count):
                mixed = mixed + coeffs[k : k + 1, :] * expand_v[slot, k * width : (k + 1) * width, :]
            out_hot = hot_from(edge_count, look_up(return_v[tile], ends_v[tile, 1] & (cap - 1)))
            sum_v[...] += dot_at(mixed.astype(jnp.bfloat16), out_hot, 1, 1)
        return carry

    lax.fori_loop(0, n // expand_v.shape[0], some_tiles, 0)
    for copy in sent:
        copy.wait_send()


def on_device(
    n,
    edge_state,
    atom_state,
    atom_sends,
    edge_source,
    edge_target,
    send_edges,
    triplet_in,
    triplet_out,
    triplet_valid,
    triplet_basis,
    return_edges,
    w_edge,
    w_source,
    w_down,
    w_bilinear,
    w_up,
    w_residual,
    w_atom,
):
    cap = triplet_in.shape[0] // n
    if cap % WIN or cap & (cap - 1) or n & (n - 1):
        return plain_on_device(
            edge_state,
            atom_state,
            atom_sends,
            edge_source,
            edge_target,
            send_edges,
            triplet_in,
            triplet_out,
            triplet_valid,
            triplet_basis,
            return_edges,
            w_edge,
            w_source,
            w_down,
            w_bilinear,
            w_up,
            w_residual,
            w_atom,
        )
    edge_count, edge_width = edge_state.shape
    atom_count, atom_width = atom_state.shape
    basis_count = triplet_basis.shape[0]
    width = w_down.shape[1]
    slots = atom_sends.shape[0] // n
    bf16 = jnp.bfloat16
    loaded = (
        atom_state,
        atom_sends.reshape(1, -1),
        edge_state,
        w_edge,
        edge_source.reshape(1, -1),
        w_source,
        w_down.T,
        w_bilinear,
        w_residual,
        send_edges.reshape(n, 1, cap),
        return_edges.reshape(n, 1, cap),
    )
    group = 4 if n % 4 == 0 else 1
    chain, total = pl.pallas_call(
        functools.partial(block_kernel, n, len(loaded)),
        out_shape=(
            jax.ShapeDtypeStruct((edge_count, edge_width), jnp.float32),
            jax.ShapeDtypeStruct((width, edge_count), jnp.float32),
        ),
        in_specs=[pl.BlockSpec(memory_space=pl.ANY)] * (len(loaded) + 4),
        out_specs=(pl.BlockSpec(memory_space=pltpu.VMEM),) * 2,
        scratch_shapes=[pltpu.VMEM(each.shape, each.dtype) for each in loaded]
        + [
            pltpu.VMEM((n, 3, 1, cap), jnp.int32),
            pltpu.VMEM((n, 3, 1, cap), jnp.int32),
            pltpu.VMEM(triplet_basis.shape, bf16),
            pltpu.VMEM((n, basis_count, cap), bf16),
            pltpu.VMEM((n, slots, atom_width), bf16),
            pltpu.VMEM((n, slots, atom_width), bf16),
            pltpu.VMEM((basis_count * width, edge_count), bf16),
            pltpu.VMEM((group, basis_count * width, cap), jnp.float32),
            pltpu.SemaphoreType.DMA((len(loaded),)),
            pltpu.SemaphoreType.DMA((4,)),
            pltpu.SemaphoreType.DMA((3, n)),
            pltpu.SemaphoreType.DMA((3, n)),
        ],
        compiler_params=pltpu.CompilerParams(collective_id=0, has_side_effects=True),
        name="block",
    )(
        *loaded,
        triplet_in.reshape(n, 1, cap),
        triplet_out.reshape(n, 1, cap),
        triplet_valid.reshape(n, 1, cap),
        triplet_basis,
    )
    return pl.pallas_call(
        tail_kernel,
        out_shape=(
            jax.ShapeDtypeStruct((edge_count, edge_width), bf16),
            jax.ShapeDtypeStruct((atom_count, atom_width), bf16),
        ),
        in_specs=[pl.BlockSpec(memory_space=pltpu.VMEM)] * 6,
        out_specs=(pl.BlockSpec(memory_space=pltpu.VMEM),) * 2,
        name="tail",
    )(total, chain, atom_state, edge_target.reshape(1, -1), w_up, w_atom)


def solution(mesh):
    placed = (
        P(("groups", "graph"), None),
        P(("groups", "graph"), None),
        P(("groups", "graph")),
        P(("groups", "graph")),
        P(("groups", "graph")),
        P(("groups", "graph")),
        P(("groups", "graph")),
        P(("groups", "graph")),
        P(("groups", "graph")),
        P(None, ("groups", "graph")),
        P(("groups", "graph")),
        P(),
        P(),
        P(),
        P(),
        P(),
        P(),
        P(),
    )
    return jax.shard_map(
        functools.partial(on_device, mesh.shape["graph"]),
        mesh=mesh,
        in_specs=placed,
        out_specs=(P(("groups", "graph"), None), P(("groups", "graph"), None)),
        check_vma=False,
    )
```

profile of v0, /device:TPU:0, one launch (start us, length us, event | category | flops | bytes accessed | tf_op | source)
XLA Modules:
  0.0 24.1 jit_solution(5839060912040603054)
XLA Ops:
  0.6 21.1 %block.1 = (f32[256,512]{1,0:T(8,128)}, f32[64,256]{1,0:T(8,128)}) custom-call(bf16[16,256]{1,0:T(8,128)(2,1)} %atom_v.1, s32[1,128]{1,0:T(1,128)} %bitcast.17, bf16[256,512]{1,0:T(8,128)(2,1)} %refs_2_.1, bf16[512,512]{1,0:T(8,128)(2,1)} %refs_3_.1, s32[1,256]{1,0:T(1,128)} %bitcast.15, bf16[256,512]{1,0:T(8,128)(2,1)} %refs_5_.1, bf16[64,512]{1,0:T(8,128)(2,1)} %bitcast.9, ...), custom_call_target="tpu_custom_call" | custom-call | tf_op jit(solution)/shard_map/block/pallas_call | solution.py:399
  21.8 2.4 %tail.1 = (bf16[256,512]{1,0:T(8,128)(2,1)}, bf16[16,256]{1,0:T(8,128)(2,1)}) custom-call(f32[64,256]{1,0:T(8,128)} %get-tuple-element.4.sum_v, f32[256,512]{1,0:T(8,128)} %get-tuple-element.5.chain_v, bf16[16,256]{1,0:T(8,128)(2,1)} %atom_v.1, s32[1,256]{1,0:T(1,128)} %bitcast.16, bf16[64,512]{1,0:T(8,128)(2,1)} %w_up_v.1, bf16[512,256]{1,0:T(8,128)(2,1)} %w_atom_v.1), custom_call_target="tpu_custom_call" | custom-call | tf_op jit(solution)/shard_map/tail/pallas_call | solution.py:431
where the time goes:
time: 24.4 us; the launch traced here: 24.1 us
  Pallas kernels  23.5 us (96%)
  between operations  0.64 us (3%)
    pallas_call x1, Pallas kernels, on_device(): pl.pallas_call(functools.partial(block_kernel, n, len(loaded)), out_shape...  21.1 us
    pallas_call x1, Pallas kernels, on_device(): pl.pallas_call(tail_kernel, out_shape=(jax.ShapeDtypeStruct((edge_count,...  2.39 us

commit v1 on v0

--- a/solution.py
+++ b/solution.py
@@ -8,6 +8,8 @@
 from jax.sharding import PartitionSpec as P
 
 WIN = 512
+APARTS = 1
+UNROLL = False
 
 
 inv_root = 0.7071067811865476
@@ -123,7 +125,8 @@
 
 
 def silu(value):
-    return value / (1.0 + jnp.exp(-value))
+    half = 0.5 * value
+    return half + half * jnp.tanh(half)
 
 
 def dot_at(left, right, left_dim, right_dim):
@@ -149,10 +152,10 @@
 
 
 def look_up(table, indices):
-    lanes = 128
+    lanes = indices.shape[1]
     found = []
-    for start in range(0, indices.shape[1], lanes):
-        wanted = jnp.broadcast_to(indices[:, start : start + lanes], (8, lanes))
+    for row in range(indices.shape[0]):
+        wanted = jnp.broadcast_to(indices[row : row + 1, :], (8, lanes))
         lane = wanted & (lanes - 1)
         value = jnp.zeros_like(wanted)
         for first in range(0, table.shape[1], lanes):
@@ -168,41 +171,46 @@
 
 
 def hot_from(row_count, eight_rows):
-    rows = lax.broadcasted_iota(jnp.int32, (row_count, eight_rows.shape[1]), 0)
-    spread = jnp.concatenate([eight_rows] * (row_count // 8), axis=0)
-    return jnp.where(rows == spread, 1.0, 0.0).astype(jnp.bfloat16)
-
-
-def tail_kernel(sum_v, chain_v, atom_v, target_v, w_up_v, w_atom_v, edge_out_ref, atom_out_ref):
-    aggregate = sum_v[...].T.astype(jnp.bfloat16)
-    update = silu(matmul(aggregate, w_up_v[...]))
-    edge_out = (chain_v[...] + update).astype(jnp.bfloat16)
-    edge_out_ref[...] = edge_out
-    contrib = matmul(edge_out, w_atom_v[...]).astype(jnp.bfloat16)
-    atom_sum = matmul(hot_columns(atom_v.shape[0], target_v[...]), contrib)
-    atom_out_ref[...] = (atom_v[...].astype(jnp.float32) + silu(0.25 * atom_sum)).astype(
-        jnp.bfloat16
-    )
+    lanes = eight_rows.shape[1]
+    sixteen = jnp.concatenate([eight_rows] * 2, axis=0).astype(jnp.int16)
+    rows = lax.broadcasted_iota(jnp.int32, (row_count, 128), 0).astype(jnp.int16)
+    spread = jnp.concatenate([sixteen] * (row_count // 16), axis=0)
+    rows = jnp.concatenate([rows] * (lanes // 128), axis=1)
+    return jnp.where(rows == spread, jnp.bfloat16(1.0), jnp.bfloat16(0.0))
+
+
+def finish(total, chain, atom, target, w_up, w_atom):
+    update = silu(dot_at(total.astype(jnp.bfloat16), w_up, 0, 0))
+    edge_out = (chain + update).astype(jnp.bfloat16)
+    contrib = matmul(edge_out, w_atom).astype(jnp.bfloat16)
+    atom_sum = matmul(hot_columns(atom.shape[0], target), contrib)
+    atom_out = (atom.astype(jnp.float32) + silu(0.25 * atom_sum)).astype(jnp.bfloat16)
+    return edge_out, atom_out
 
 
 def block_kernel(n, loaded, *refs):
     sources = refs[:loaded]
     in_hbm, out_hbm, valid_hbm, basis_hbm = refs[loaded : loaded + 4]
-    chain_v, sum_v = refs[loaded + 4 : loaded + 6]
+    edge_out_ref, atom_out_ref = refs[loaded + 4 : loaded + 6]
     held = refs[loaded + 6 : 2 * loaded + 6]
     (
         stage_v,
+        valid_v,
+        stage_basis_v,
+        ends_out,
         ends_v,
-        stage_basis_v,
+        basis_out,
         basis_v,
         atoms_out,
         atoms_in,
-        table_v,
-        expand_v,
+        weight_v,
+        chain_v,
+        sum_v,
         load_sem,
         stage_sem,
         send_sem,
         recv_sem,
+        ready,
     ) = refs[2 * loaded + 6 :]
     (
         atom_v,
@@ -216,121 +224,207 @@
         w_res_v,
         send_v,
         return_v,
+        target_v,
+        w_up_v,
+        w_atom_v,
     ) = held
     me = lax.axis_index("graph")
-    cap = ends_v.shape[3]
+    cap = basis_v.shape[2]
+    rows = ends_v.shape[1] // 2
     edge_count = edge_v.shape[0]
     width = w_down_v.shape[0]
     basis_count = basis_v.shape[1]
+    bf16 = jnp.bfloat16
+    layers = ready.shape[0]
+    span = n // layers
+    layer = lax.div(me, span)
+    arrays = (ends_v, basis_v, atoms_in)
+    sources_of = (ends_out, basis_out, atoms_out)
+
+    def signal(semaphore, peer):
+        pl.semaphore_signal(
+            semaphore, inc=1, device_id={"graph": peer}, device_id_type=pl.DeviceIdType.MESH
+        )
 
     barrier = pltpu.get_barrier_semaphore()
-    for step in range(1, n):
-        pl.semaphore_signal(
-            barrier,
-            inc=1,
-            device_id={"graph": partner(me, step, n)},
-            device_id_type=pl.DeviceIdType.MESH,
-        )
     loads = [
         pltpu.make_async_copy(src, dst, load_sem.at[i])
         for i, (src, dst) in enumerate(zip(sources, held))
     ]
-    for load in loads:
+    stages = [
+        pltpu.make_async_copy(src, dst, stage_sem.at[i])
+        for i, (src, dst) in enumerate(
+            (
+                (in_hbm, stage_v.at[:, pl.ds(0, rows)]),
+                (out_hbm, stage_v.at[:, pl.ds(rows, rows)]),
+                (valid_hbm, valid_v),
+                (basis_hbm, stage_basis_v),
+            )
+        )
+    ]
+    for load in loads[:2]:
         load.start()
-    stages = [
-        pltpu.make_async_copy(src, stage_v.at[:, i], stage_sem.at[i])
-        for i, src in enumerate((in_hbm, out_hbm, valid_hbm))
-    ]
-    stages.append(pltpu.make_async_copy(basis_hbm, stage_basis_v, stage_sem.at[3]))
+    for peer in range(n):
+        pl.when((layer <= peer // span) & (me != peer))(functools.partial(signal, barrier, peer))
     for stage in stages:
         stage.start()
+    for load in loads[2:]:
+        load.start()
+    pl.semaphore_wait(barrier, span * (layer + 1) - 1)
+    for peer in range(n):
+        pl.when(layer > peer // span)(functools.partial(signal, ready.at[layer], peer))
     loads[0].wait()
     loads[1].wait()
     picked = dot_at(hot_columns(atom_v.shape[0], asend_v[...]), atom_v[...], 0, 0)
-    atoms_out[...] = picked.reshape(atoms_out.shape).astype(jnp.bfloat16)
-    pl.semaphore_wait(barrier, n - 1)
-
-    def parts(peer):
-        lanes = pl.ds(pl.multiple_of(peer * cap, cap), cap)
-        return (
-            (atoms_out.at[peer], atoms_in.at[me]),
-            (stage_v.at[peer], ends_v.at[me]),
-            (stage_basis_v.at[:, lanes], basis_v.at[me]),
-        )
-
-    sent = []
-    for kinds in ((0,), (1, 2)):
-        if kinds[0]:
-            for stage in stages:
-                stage.wait()
-        for step in range(n):
-            peer = partner(me, step, n)
-            for kind in kinds:
-                src, dst = parts(peer)[kind]
-                if step == 0:
-                    copy = pltpu.make_async_copy(src, dst, recv_sem.at[kind, step])
-                else:
-                    copy = pltpu.make_async_remote_copy(
-                        src_ref=src,
-                        dst_ref=dst,
-                        send_sem=send_sem.at[kind, step],
-                        recv_sem=recv_sem.at[kind, step],
+    atoms_out[...] = picked.reshape(atoms_out.shape).astype(bf16)
+    def own(kind):
+        pltpu.make_async_copy(
+            sources_of[kind].at[me], arrays[kind].at[me], recv_sem.at[kind, 0]
+        ).start()
+
+    inner = lax.rem(me, span)
+
+    def send(kinds, other):
+        apart = partner(layer, other, layers)
+        for step in range(span):
+            peer = other * span + partner(inner, step, span)
+
+            def start():
+                for kind in kinds:
+                    pltpu.make_async_remote_copy(
+                        src_ref=sources_of[kind].at[peer],
+                        dst_ref=arrays[kind].at[me],
+                        send_sem=send_sem.at[kind, other],
+                        recv_sem=recv_sem.at[kind, 0 if kind == 2 else apart],
                         device_id={"graph": peer},
                         device_id_type=pl.DeviceIdType.MESH,
-                    )
-                    sent.append(copy)
-                copy.start()
-
-    def arrive(kind, buffer, step, peer):
-        pltpu.make_async_copy(buffer.at[peer], buffer.at[peer], recv_sem.at[kind, step]).wait()
-
-    for load in loads[2:7]:
+                    ).start()
+
+            if step:
+                start()
+            else:
+                pl.when(layer != other)(start)
+
+    def sent(kind, other):
+        buffer = arrays[kind]
+
+        @pl.when(layer != other)
+        def _():
+            arrive(buffer.at[pl.ds(0, span)], send_sem.at[kind, other])
+
+        @pl.when(layer == other)
+        def _():
+            arrive(buffer.at[pl.ds(0, span - 1)], send_sem.at[kind, other])
+
+    def arrive(buffer, sem):
+        pltpu.make_async_copy(buffer, buffer, sem).wait()
+
+    own(2)
+    for other in range(layers):
+
+        @pl.when(layer >= other)
+        def _():
+            send((2,), other)
+
+    for stage in stages:
+        stage.wait()
+    ends_out[...] = stage_v[...].astype(jnp.int16)
+    for tile in range(n):
+        basis_out[tile] = stage_basis_v[:, tile * cap : (tile + 1) * cap] * valid_v[tile].astype(
+            jnp.float32
+        ).astype(bf16)
+    own(0)
+    own(1)
+    for other in range(layers):
+
+        @pl.when(layer == other)
+        def _():
+            send((0, 1), other)
+
+    for other in range(layers):
+
+        @pl.when(layer > other)
+        def _():
+            send((0, 1), other)
+
+    for load in loads[2:8]:
         load.wait()
+    weight_v[...] = jnp.concatenate(
+        [w_bilinear_v[:, k * width : (k + 1) * width] for k in range(basis_count)], axis=0
+    ).T
     edge = edge_v[...]
     pre_act = matmul(edge, w_edge_v[...])
     pick = hot_columns(atoms_in.shape[0] * atoms_in.shape[1], source_v[...])
-    for step in range(n):
-        arrive(0, atoms_in, step, partner(me, step, n))
-    arrived = atoms_in[...].astype(jnp.float32).reshape(pick.shape[0], -1).astype(jnp.bfloat16)
-    src_rows = dot_at(pick, arrived, 0, 0).astype(jnp.bfloat16)
-    activated = silu(pre_act + matmul(src_rows, w_source_v[...])).astype(jnp.bfloat16)
-    projected = silu(dot_at(activated, w_down_v[...], 1, 1)).astype(jnp.bfloat16)
-    for load in loads[7:]:
+    for load in loads[8:]:
         load.wait()
-    table_v[...] = dot_at(w_bilinear_v[...], projected, 0, 1).astype(jnp.bfloat16)
-    base = ((edge.astype(jnp.float32) + activated.astype(jnp.float32)) * inv_root).astype(
-        jnp.bfloat16
-    )
-    inner_one = silu(matmul(base, w_res_v[0])).astype(jnp.bfloat16)
-    middle = ((base.astype(jnp.float32) + silu(matmul(inner_one, w_res_v[1]))) * inv_root).astype(
-        jnp.bfloat16
-    )
-    inner_two = silu(matmul(middle, w_res_v[2])).astype(jnp.bfloat16)
+    for other in range(1, layers):
+
+        @pl.when(layer < other)
+        def _():
+            pl.semaphore_wait(ready.at[other], span)
+            send((2,), other)
+
+        @pl.when(layer + 1 == other)
+        def _():
+            send((0, 1), other)
+
+    for other in range(2, layers):
+
+        @pl.when(layer + 1 < other)
+        def _():
+            send((0, 1), other)
+
+    arrive(atoms_in, recv_sem.at[2, 0])
+    arrived = atoms_in[...].astype(jnp.float32).reshape(pick.shape[0], -1).astype(bf16)
+    src_rows = dot_at(pick, arrived, 0, 0).astype(bf16)
+    activated = silu(pre_act + matmul(src_rows, w_source_v[...])).astype(bf16)
+    projected = silu(dot_at(w_down_v[...], activated, 1, 1)).astype(bf16)
+    base = ((edge.astype(jnp.float32) + activated.astype(jnp.float32)) * inv_root).astype(bf16)
+    inner_one = silu(matmul(base, w_res_v[0])).astype(bf16)
+    middle = ((base.astype(jnp.float32) + silu(matmul(inner_one, w_res_v[1]))) * inv_root).astype(bf16)
+    inner_two = silu(matmul(middle, w_res_v[2])).astype(bf16)
     chain_v[...] = (middle.astype(jnp.float32) + silu(matmul(inner_two, w_res_v[3]))) * inv_root
+
+    def gather(tile):
+        ends = ends_v[tile].astype(jnp.int32) & (cap - 1)
+        in_hot = hot_from(edge_count, look_up(send_v[tile], ends[:rows]))
+        gathered = matmul(projected, in_hot).astype(bf16)
+        coeffs = basis_v[tile].astype(jnp.float32)
+        terms = []
+        for k in range(basis_count):
+            spread = jnp.broadcast_to(coeffs[k : k + 1, :], (16, cap)).astype(bf16)
+            terms.append(jnp.concatenate([spread] * (width // 16), axis=0) * gathered)
+        out_hot = hot_from(edge_count, look_up(return_v[tile], ends[rows:]))
+        return jnp.concatenate(terms, axis=0), out_hot
+
     sum_v[...] = jnp.zeros_like(sum_v)
 
     def some_tiles(group, carry):
-        tiles = []
-        for slot in range(expand_v.shape[0]):
-            step = group * expand_v.shape[0] + slot
-            tile = partner(me, step, n)
-            tiles.append(tile)
-            arrive(1, ends_v, step, tile)
-            arrive(2, basis_v, step, tile)
-        for slot, tile in enumerate(tiles):
-            in_hot = hot_from(edge_count, look_up(send_v[tile], ends_v[tile, 0] & (cap - 1)))
-            expand_v[slot] = matmul(table_v[...], in_hot)
-            coeffs = basis_v[tile].astype(jnp.float32) * ends_v[tile, 2].astype(jnp.float32)
-            mixed = jnp.zeros((width, cap), jnp.float32)
-            for k in range(basis_count):
-                mixed = mixed + coeffs[k : k + 1, :] * expand_v[slot, k * width : (k + 1) * width, :]
-            out_hot = hot_from(edge_count, look_up(return_v[tile], ends_v[tile, 1] & (cap - 1)))
-            sum_v[...] += dot_at(mixed.astype(jnp.bfloat16), out_hot, 1, 1)
+        for i in range(APARTS):
+            apart = group * APARTS + i
+            first = partner(layer, apart, layers) * span
+            for kind, buffer in enumerate(arrays[:2]):
+                arrive(buffer.at[pl.ds(first, span)], recv_sem.at[kind, apart])
+        pairs = [gather(partner(me, group * APARTS * span + i, n)) for i in range(APARTS * span)]
+        terms = jnp.concatenate([pair[0] for pair in pairs], axis=1)
+        hots = jnp.concatenate([pair[1] for pair in pairs], axis=1)
+        sum_v[...] += dot_at(terms, hots, 1, 1)
         return carry
 
-    lax.fori_loop(0, n // expand_v.shape[0], some_tiles, 0)
-    for copy in sent:
-        copy.wait_send()
+    if UNROLL:
+        for group in range(layers // APARTS):
+            some_tiles(group, 0)
+    else:
+        lax.fori_loop(0, layers // APARTS, some_tiles, 0)
+    total = matmul(weight_v[...], sum_v[...].astype(bf16))
+    edge_out, atom_out = finish(
+        total, chain_v[...], atom_v[...], target_v[...], w_up_v[...], w_atom_v[...]
+    )
+    edge_out_ref[...] = edge_out
+    atom_out_ref[...] = atom_out
+    for other in range(layers):
+        for kind in range(3):
+            sent(kind, other)
 
 
 def on_device(
@@ -355,7 +449,8 @@
     w_atom,
 ):
     cap = triplet_in.shape[0] // n
-    if cap % WIN or cap & (cap - 1) or n & (n - 1):
+    layers = 4
+    if cap % WIN or cap & (cap - 1) or n & (n - 1) or n < layers:
         return plain_on_device(
             edge_state,
             atom_state,
@@ -394,50 +489,48 @@
         w_residual,
         send_edges.reshape(n, 1, cap),
         return_edges.reshape(n, 1, cap),
-    )
-    group = 4 if n % 4 == 0 else 1
-    chain, total = pl.pallas_call(
+        edge_target.reshape(1, -1),
+        w_up,
+        w_atom,
+    )
+    whole = pl.BlockSpec(memory_space=pltpu.VMEM)
+    return pl.pallas_call(
         functools.partial(block_kernel, n, len(loaded)),
         out_shape=(
-            jax.ShapeDtypeStruct((edge_count, edge_width), jnp.float32),
-            jax.ShapeDtypeStruct((width, edge_count), jnp.float32),
+            pltpu.VMEM((edge_count, edge_width), bf16),
+            pltpu.VMEM((atom_count, atom_width), bf16),
         ),
         in_specs=[pl.BlockSpec(memory_space=pl.ANY)] * (len(loaded) + 4),
-        out_specs=(pl.BlockSpec(memory_space=pltpu.VMEM),) * 2,
+        out_specs=(whole, whole),
         scratch_shapes=[pltpu.VMEM(each.shape, each.dtype) for each in loaded]
         + [
-            pltpu.VMEM((n, 3, 1, cap), jnp.int32),
-            pltpu.VMEM((n, 3, 1, cap), jnp.int32),
+            pltpu.VMEM((n, 2 * (cap // 128), 128), jnp.int32),
+            pltpu.VMEM((n, 1, cap), jnp.int32),
             pltpu.VMEM(triplet_basis.shape, bf16),
+            pltpu.VMEM((n, 2 * (cap // 128), 128), jnp.int16),
+            pltpu.VMEM((n, 2 * (cap // 128), 128), jnp.int16),
+            pltpu.VMEM((n, basis_count, cap), bf16),
             pltpu.VMEM((n, basis_count, cap), bf16),
             pltpu.VMEM((n, slots, atom_width), bf16),
             pltpu.VMEM((n, slots, atom_width), bf16),
-            pltpu.VMEM((basis_count * width, edge_count), bf16),
-            pltpu.VMEM((group, basis_count * width, cap), jnp.float32),
+            pltpu.VMEM((width, basis_count * width), bf16),
+            pltpu.VMEM((edge_count, edge_width), jnp.float32),
+            pltpu.VMEM((basis_count * width, edge_count), jnp.float32),
             pltpu.SemaphoreType.DMA((len(loaded),)),
             pltpu.SemaphoreType.DMA((4,)),
-            pltpu.SemaphoreType.DMA((3, n)),
-            pltpu.SemaphoreType.DMA((3, n)),
+            pltpu.SemaphoreType.DMA((3, layers)),
+            pltpu.SemaphoreType.DMA((3, layers)),
+            pltpu.SemaphoreType.REGULAR((layers,)),
         ],
         compiler_params=pltpu.CompilerParams(collective_id=0, has_side_effects=True),
         name="block",
     )(
         *loaded,
-        triplet_in.reshape(n, 1, cap),
-        triplet_out.reshape(n, 1, cap),
+        triplet_in.reshape(n, cap // 128, 128),
+        triplet_out.reshape(n, cap // 128, 128),
         triplet_valid.reshape(n, 1, cap),
         triplet_basis,
     )
-    return pl.pallas_call(
-        tail_kernel,
-        out_shape=(
-            jax.ShapeDtypeStruct((edge_count, edge_width), bf16),
-            jax.ShapeDtypeStruct((atom_count, atom_width), bf16),
-        ),
-        in_specs=[pl.BlockSpec(memory_space=pltpu.VMEM)] * 6,
-        out_specs=(pl.BlockSpec(memory_space=pltpu.VMEM),) * 2,
-        name="tail",
-    )(total, chain, atom_state, edge_target.reshape(1, -1), w_up, w_atom)
 
 
 def solution(mesh):

time: 24.4 us -> 23.7 us (0.971)
  the two profiles are of different devices: /device:TPU:0 before, /device:TPU:29 now
where the time goes in v1:
time: 23.7 us; the launch traced here: 23.6 us
  Pallas kernels  21.6 us (91%)
  local copies, waits for them, and re-layouts  1.3 us (5%)
  between operations  0.65 us (3%)
    pallas_call x1, Pallas kernels, on_device(): pl.pallas_call(functools.partial(block_kernel, n, len(loaded)), out_shape...  21.6 us
    unnamed x2, local copies, waits for them, and re-layouts  1.3 us

profile of v1, /device:TPU:29, one launch (start us, length us, event | category | flops | bytes accessed | tf_op | source)
XLA Modules:
  0.0 23.6 jit_solution(16439226401713798445)
XLA Ops:
  0.6 21.6 %block.1 = (bf16[256,512]{1,0:T(8,128)(2,1)S(1)}, bf16[16,256]{1,0:T(8,128)(2,1)S(1)}) custom-call(bf16[16,256]{1,0:T(8,128)(2,1)} %refs_0_.1, s32[1,128]{1,0:T(1,128)} %bitcast.17, bf16[256,512]{1,0:T(8,128)(2,1)} %refs_2_.1, bf16[512,512]{1,0:T(8,128)(2,1)} %refs_3_.1, s32[1,256]{1,0:T(1,128)} %bitcast.15, bf16[256,512]{1,0:T(8,128)(2,1)} %refs_5_.1, ...), custom_call_target="tpu_custom_call" | custom-call | tf_op jit(solution)/shard_map/block/pallas_call | solution.py:497
  22.3 0.7 %copy.22 = bf16[256,512]{1,0:T(8,128)(2,1)} copy(bf16[256,512]{1,0:T(8,128)(2,1)S(1)} %get-tuple-element.2) | data formatting | bytes 524288
  23.0 0.6 %copy.23 = bf16[16,256]{1,0:T(8,128)(2,1)} copy(bf16[16,256]{1,0:T(8,128)(2,1)S(1)} %get-tuple-element.3) | data formatting | bytes 16384

commit v2 on v1

--- a/solution.py
+++ b/solution.py
@@ -364,13 +364,9 @@
             pl.semaphore_wait(ready.at[other], span)
             send((2,), other)
 
-        @pl.when(layer + 1 == other)
-        def _():
-            send((0, 1), other)
-
-    for other in range(2, layers):
-
-        @pl.when(layer + 1 < other)
+    for other in range(1, layers):
+
+        @pl.when(layer < other)
         def _():
             send((0, 1), other)
 

time: 23.7 us -> 20.3 us (0.86)
  Pallas kernels: 21.6 us -> 18.2 us
    pallas_call x1, Pallas kernels: 21.6 us -> 18.2 us  [on_device(): pl.pallas_call(functools.partial(block_kernel, n, len(loaded)), out_shape...]
where the time goes in v2:
time: 20.3 us; the launch traced here: 20.1 us
  Pallas kernels  18.2 us (90%)
  local copies, waits for them, and re-layouts  1.3 us (6%)
  between operations  0.65 us (3%)
    pallas_call x1, Pallas kernels, on_device(): pl.pallas_call(functools.partial(block_kernel, n, len(loaded)), out_shape...  18.2 us
    unnamed x2, local copies, waits for them, and re-layouts  1.3 us

profile of v2, /device:TPU:29, one launch (start us, length us, event | category | flops | bytes accessed | tf_op | source)
XLA Modules:
  0.0 20.1 jit_solution(14375808264372724313)
XLA Ops:
  0.6 18.2 %block.1 = (bf16[256,512]{1,0:T(8,128)(2,1)S(1)}, bf16[16,256]{1,0:T(8,128)(2,1)S(1)}) custom-call(bf16[16,256]{1,0:T(8,128)(2,1)} %refs_0_.1, s32[1,128]{1,0:T(1,128)} %bitcast.17, bf16[256,512]{1,0:T(8,128)(2,1)} %refs_2_.1, bf16[512,512]{1,0:T(8,128)(2,1)} %refs_3_.1, s32[1,256]{1,0:T(1,128)} %bitcast.15, bf16[256,512]{1,0:T(8,128)(2,1)} %refs_5_.1, ...), custom_call_target="tpu_custom_call" | custom-call | tf_op jit(solution)/shard_map/block/pallas_call | solution.py:493
  18.8 0.7 %copy.22 = bf16[256,512]{1,0:T(8,128)(2,1)} copy(bf16[256,512]{1,0:T(8,128)(2,1)S(1)} %get-tuple-element.2) | data formatting | bytes 524288
  19.5 0.6 %copy.23 = bf16[16,256]{1,0:T(8,128)(2,1)} copy(bf16[16,256]{1,0:T(8,128)(2,1)S(1)} %get-tuple-element.3) | data formatting | bytes 16384

commit v3 on v2

--- a/solution.py
+++ b/solution.py
@@ -186,6 +186,17 @@
     atom_sum = matmul(hot_columns(atom.shape[0], target), contrib)
     atom_out = (atom.astype(jnp.float32) + silu(0.25 * atom_sum)).astype(jnp.bfloat16)
     return edge_out, atom_out
+
+
+def put_out(edge_v, atom_v, edge_out, atom_out, sem):
+    puts = [
+        pltpu.make_async_copy(edge_v, edge_out, sem.at[0]),
+        pltpu.make_async_copy(atom_v, atom_out, sem.at[1]),
+    ]
+    for put in puts:
+        put.start()
+    for put in puts:
+        put.wait()
 
 
 def block_kernel(n, loaded, *refs):
@@ -490,7 +501,7 @@
         w_atom,
     )
     whole = pl.BlockSpec(memory_space=pltpu.VMEM)
-    return pl.pallas_call(
+    edge_out, atom_out = pl.pallas_call(
         functools.partial(block_kernel, n, len(loaded)),
         out_shape=(
             pltpu.VMEM((edge_count, edge_width), bf16),
@@ -527,6 +538,20 @@
         triplet_valid.reshape(n, 1, cap),
         triplet_basis,
     )
+    return pl.pallas_call(
+        put_out,
+        out_shape=(
+            jax.ShapeDtypeStruct(edge_out.shape, bf16),
+            jax.ShapeDtypeStruct(atom_out.shape, bf16),
+        ),
+        in_specs=[whole, whole],
+        out_specs=(pl.BlockSpec(memory_space=pl.ANY),) * 2,
+        scratch_shapes=[pltpu.SemaphoreType.DMA((2,))],
+        name="tail",
+    )(
+        pltpu.with_memory_space_constraint(edge_out, pltpu.VMEM),
+        pltpu.with_memory_space_constraint(atom_out, pltpu.VMEM),
+    )
 
 
 def solution(mesh):

time: 20.3 us -> 19.7 us (0.970)
  local copies, waits for them, and re-layouts: 1.3 us -> 0 us
  Pallas kernels: 18.2 us -> 18.9 us
    unnamed x2 -> x0, local copies, waits for them, and re-layouts: 1.3 us -> none
    pallas_call x0 -> x1, Pallas kernels: none -> 0.72 us  [on_device(): pl.pallas_call(put_out, out_shape=(jax.ShapeDtypeStruct(edge_out.shape, b...]
where the time goes in v3:
time: 19.7 us; the launch traced here: 19.5 us
  Pallas kernels  18.9 us (96%)
  between operations  0.65 us (3%)
    pallas_call x1, Pallas kernels, on_device(): pl.pallas_call(functools.partial(block_kernel, n, len(loaded)), out_shape...  18.2 us
    pallas_call x1, Pallas kernels, on_device(): pl.pallas_call(put_out, out_shape=(jax.ShapeDtypeStruct(edge_out.shape, b...  0.72 us

profile of v3, /device:TPU:29, one launch (start us, length us, event | category | flops | bytes accessed | tf_op | source)
XLA Modules:
  0.0 19.5 jit_solution(16445595454184126459)
XLA Ops:
  0.6 18.2 %block.1 = (bf16[256,512]{1,0:T(8,128)(2,1)S(1)}, bf16[16,256]{1,0:T(8,128)(2,1)S(1)}) custom-call(bf16[16,256]{1,0:T(8,128)(2,1)} %refs_0_.1, s32[1,128]{1,0:T(1,128)} %bitcast.17, bf16[256,512]{1,0:T(8,128)(2,1)} %refs_2_.1, bf16[512,512]{1,0:T(8,128)(2,1)} %refs_3_.1, s32[1,256]{1,0:T(1,128)} %bitcast.15, bf16[256,512]{1,0:T(8,128)(2,1)} %refs_5_.1, ...), custom_call_target="tpu_custom_call" | custom-call | tf_op jit(solution)/shard_map/block/pallas_call | solution.py:504
  18.8 0.7 %tail.1 = (bf16[256,512]{1,0:T(8,128)(2,1)}, bf16[16,256]{1,0:T(8,128)(2,1)}) custom-call(bf16[256,512]{1,0:T(8,128)(2,1)S(1)} %get-tuple-element.4.edge_v, bf16[16,256]{1,0:T(8,128)(2,1)S(1)} %get-tuple-element.5.atom_v), custom_call_target="tpu_custom_call" | custom-call | tf_op jit(solution)/shard_map/tail/pallas_call | solution.py:541

commit v4 on v3

--- a/solution.py
+++ b/solution.py
@@ -8,8 +8,7 @@
 from jax.sharding import PartitionSpec as P
 
 WIN = 512
-APARTS = 1
-UNROLL = False
+HALVES = 2
 
 
 inv_root = 0.7071067811865476
@@ -170,6 +169,28 @@
     return jnp.concatenate(found, axis=1)
 
 
+def pick_columns(table, indices):
+    lanes = 128
+    found = []
+    for start in range(0, indices.shape[1], lanes):
+        wanted = indices[:, start : start + lanes]
+        lane = wanted & (lanes - 1)
+        blocks = []
+        for row in range(0, table.shape[0], 8):
+            value = None
+            for first in range(0, table.shape[1], lanes):
+                part = jnp.take_along_axis(
+                    table[row : row + 8, first : first + lanes],
+                    lane,
+                    axis=1,
+                    mode="promise_in_bounds",
+                )
+                value = part if value is None else jnp.where(wanted - lane == first, part, value)
+            blocks.append(value)
+        found.append(jnp.concatenate(blocks, axis=0))
+    return jnp.concatenate(found, axis=1)
+
+
 def hot_from(row_count, eight_rows):
     lanes = eight_rows.shape[1]
     sixteen = jnp.concatenate([eight_rows] * 2, axis=0).astype(jnp.int16)
@@ -215,6 +236,10 @@
         atoms_out,
         atoms_in,
         weight_v,
+        rows_even,
+        rows_odd,
+        hots_even,
+        hots_odd,
         chain_v,
         sum_v,
         load_sem,
@@ -249,6 +274,8 @@
     layers = ready.shape[0]
     span = n // layers
     layer = lax.div(me, span)
+    rows_v = (rows_even, rows_odd)
+    hots_v = (hots_even, hots_odd)
     arrays = (ends_v, basis_v, atoms_in)
     sources_of = (ends_out, basis_out, atoms_out)
 
@@ -275,10 +302,10 @@
     ]
     for load in loads[:2]:
         load.start()
+    for stage in stages:
+        stage.start()
     for peer in range(n):
         pl.when((layer <= peer // span) & (me != peer))(functools.partial(signal, barrier, peer))
-    for stage in stages:
-        stage.start()
     for load in loads[2:]:
         load.start()
     pl.semaphore_wait(barrier, span * (layer + 1) - 1)
@@ -305,7 +332,7 @@
                     pltpu.make_async_remote_copy(
                         src_ref=sources_of[kind].at[peer],
                         dst_ref=arrays[kind].at[me],
-                        send_sem=send_sem.at[kind, other],
+                        send_sem=send_sem.at[kind],
                         recv_sem=recv_sem.at[kind, 0 if kind == 2 else apart],
                         device_id={"graph": peer},
                         device_id_type=pl.DeviceIdType.MESH,
@@ -315,17 +342,6 @@
                 start()
             else:
                 pl.when(layer != other)(start)
-
-    def sent(kind, other):
-        buffer = arrays[kind]
-
-        @pl.when(layer != other)
-        def _():
-            arrive(buffer.at[pl.ds(0, span)], send_sem.at[kind, other])
-
-        @pl.when(layer == other)
-        def _():
-            arrive(buffer.at[pl.ds(0, span - 1)], send_sem.at[kind, other])
 
     def arrive(buffer, sem):
         pltpu.make_async_copy(buffer, buffer, sem).wait()
@@ -382,6 +398,8 @@
             send((0, 1), other)
 
     arrive(atoms_in, recv_sem.at[2, 0])
+    for kind, buffer in enumerate(arrays[:2]):
+        arrive(buffer.at[pl.ds(layer * span, span)], recv_sem.at[kind, 0])
     arrived = atoms_in[...].astype(jnp.float32).reshape(pick.shape[0], -1).astype(bf16)
     src_rows = dot_at(pick, arrived, 0, 0).astype(bf16)
     activated = silu(pre_act + matmul(src_rows, w_source_v[...])).astype(bf16)
@@ -392,46 +410,56 @@
     inner_two = silu(matmul(middle, w_res_v[2])).astype(bf16)
     chain_v[...] = (middle.astype(jnp.float32) + silu(matmul(inner_two, w_res_v[3]))) * inv_root
 
-    def gather(tile):
-        ends = ends_v[tile].astype(jnp.int32) & (cap - 1)
-        in_hot = hot_from(edge_count, look_up(send_v[tile], ends[:rows]))
-        gathered = matmul(projected, in_hot).astype(bf16)
-        coeffs = basis_v[tile].astype(jnp.float32)
-        terms = []
-        for k in range(basis_count):
-            spread = jnp.broadcast_to(coeffs[k : k + 1, :], (16, cap)).astype(bf16)
-            terms.append(jnp.concatenate([spread] * (width // 16), axis=0) * gathered)
-        out_hot = hot_from(edge_count, look_up(return_v[tile], ends[rows:]))
-        return jnp.concatenate(terms, axis=0), out_hot
-
-    sum_v[...] = jnp.zeros_like(sum_v)
-
-    def some_tiles(group, carry):
-        for i in range(APARTS):
-            apart = group * APARTS + i
-            first = partner(layer, apart, layers) * span
-            for kind, buffer in enumerate(arrays[:2]):
-                arrive(buffer.at[pl.ds(first, span)], recv_sem.at[kind, apart])
-        pairs = [gather(partner(me, group * APARTS * span + i, n)) for i in range(APARTS * span)]
-        terms = jnp.concatenate([pair[0] for pair in pairs], axis=1)
-        hots = jnp.concatenate([pair[1] for pair in pairs], axis=1)
-        sum_v[...] += dot_at(terms, hots, 1, 1)
-        return carry
-
-    if UNROLL:
-        for group in range(layers // APARTS):
-            some_tiles(group, 0)
-    else:
-        lax.fori_loop(0, layers // APARTS, some_tiles, 0)
+    def first_of(apart):
+        return partner(layer, apart, layers) * span
+
+    def prepare(apart):
+        for i in range(span):
+            tile = first_of(apart) + i
+            ends = ends_v[tile].astype(jnp.int32) & (cap - 1)
+            edges = look_up(send_v[tile], ends[:rows])
+            rows_v[apart % 2][i] = pick_columns(projected.astype(jnp.float32), edges).astype(bf16)
+            targets = look_up(return_v[tile], ends[rows:])
+            hots_v[apart % 2][i] = hot_from(edge_count, targets)
+
+    def add_terms(apart):
+        share = basis_count // HALVES
+        hots = jnp.concatenate([hots_v[apart % 2][i] for i in range(span)], axis=1)
+        for half in range(HALVES):
+            all_terms = []
+            for i in range(span):
+                gathered = rows_v[apart % 2][i]
+                coeffs = basis_v[first_of(apart) + i].astype(jnp.float32)
+                terms = []
+                for k in range(half * share, (half + 1) * share):
+                    spread = jnp.broadcast_to(coeffs[k : k + 1, :], (16, cap)).astype(bf16)
+                    terms.append(jnp.concatenate([spread] * (width // 16), axis=0) * gathered)
+                all_terms.append(jnp.concatenate(terms, axis=0))
+            part = dot_at(jnp.concatenate(all_terms, axis=1), hots, 1, 1)
+            slots = pl.ds(half * share * width, share * width)
+            if apart:
+                sum_v[slots, :] += part
+            else:
+                sum_v[slots, :] = part
+
+    def arrived_from(apart):
+        for kind, buffer in enumerate(arrays[:2]):
+            arrive(buffer.at[pl.ds(first_of(apart), span)], recv_sem.at[kind, apart])
+
+    prepare(0)
+    for apart in range(layers):
+        add_terms(apart)
+        if apart + 1 < layers:
+            arrived_from(apart + 1)
+            prepare(apart + 1)
     total = matmul(weight_v[...], sum_v[...].astype(bf16))
     edge_out, atom_out = finish(
         total, chain_v[...], atom_v[...], target_v[...], w_up_v[...], w_atom_v[...]
     )
     edge_out_ref[...] = edge_out
     atom_out_ref[...] = atom_out
-    for other in range(layers):
-        for kind in range(3):
-            sent(kind, other)
+    for kind, buffer in enumerate(arrays):
+        arrive(buffer.at[pl.ds(0, n - 1)], send_sem.at[kind])
 
 
 def on_device(
@@ -521,11 +549,15 @@
             pltpu.VMEM((n, slots, atom_width), bf16),
             pltpu.VMEM((n, slots, atom_width), bf16),
             pltpu.VMEM((width, basis_count * width), bf16),
+            pltpu.VMEM((n // layers, width, cap), bf16),
+            pltpu.VMEM((n // layers, width, cap), bf16),
+            pltpu.VMEM((n // layers, edge_count, cap), bf16),
+            pltpu.VMEM((n // layers, edge_count, cap), bf16),
             pltpu.VMEM((edge_count, edge_width), jnp.float32),
             pltpu.VMEM((basis_count * width, edge_count), jnp.float32),
             pltpu.SemaphoreType.DMA((len(loaded),)),
             pltpu.SemaphoreType.DMA((4,)),
-            pltpu.SemaphoreType.DMA((3, layers)),
+            pltpu.SemaphoreType.DMA((3,)),
             pltpu.SemaphoreType.DMA((3, layers)),
             pltpu.SemaphoreType.REGULAR((layers,)),
         ],

time: 19.7 us -> 19.4 us (0.985)
  Pallas kernels: 18.9 us -> 18.6 us
    pallas_call x1, Pallas kernels: 18.2 us -> 17.8 us  [on_device(): pl.pallas_call(functools.partial(block_kernel, n, len(loaded)), out_shape...]
where the time goes in v4:
time: 19.4 us; the launch traced here: 19.2 us
  Pallas kernels  18.6 us (96%)
  between operations  0.65 us (3%)
    pallas_call x1, Pallas kernels, on_device(): pl.pallas_call(functools.partial(block_kernel, n, len(loaded)), out_shape...  17.8 us
    pallas_call x1, Pallas kernels, on_device(): pl.pallas_call(put_out, out_shape=(jax.ShapeDtypeStruct(edge_out.shape, b...  0.72 us

profile of v4, /device:TPU:29, one launch (start us, length us, event | category | flops | bytes accessed | tf_op | source)
XLA Modules:
  0.0 19.2 jit_solution(11822452282942420161)
XLA Ops:
  0.6 17.8 %block.1 = (bf16[256,512]{1,0:T(8,128)(2,1)S(1)}, bf16[16,256]{1,0:T(8,128)(2,1)S(1)}) custom-call(bf16[16,256]{1,0:T(8,128)(2,1)} %refs_0_.1, s32[1,128]{1,0:T(1,128)} %bitcast.17, bf16[256,512]{1,0:T(8,128)(2,1)} %refs_2_.1, bf16[512,512]{1,0:T(8,128)(2,1)} %refs_3_.1, s32[1,256]{1,0:T(1,128)} %bitcast.15, bf16[256,512]{1,0:T(8,128)(2,1)} %refs_5_.1, ...), custom_call_target="tpu_custom_call" | custom-call | tf_op jit(solution)/shard_map/block/pallas_call | solution.py:532
  18.5 0.7 %tail.1 = (bf16[256,512]{1,0:T(8,128)(2,1)}, bf16[16,256]{1,0:T(8,128)(2,1)}) custom-call(bf16[256,512]{1,0:T(8,128)(2,1)S(1)} %get-tuple-element.4.edge_v, bf16[16,256]{1,0:T(8,128)(2,1)S(1)} %get-tuple-element.5.atom_v), custom_call_target="tpu_custom_call" | custom-call | tf_op jit(solution)/shard_map/tail/pallas_call | solution.py:573

commit v5 on v4

--- a/solution.py
+++ b/solution.py
@@ -391,7 +391,7 @@
             pl.semaphore_wait(ready.at[other], span)
             send((2,), other)
 
-    for other in range(1, layers):
+    for other in (layers - 1, *range(1, layers - 1)):
 
         @pl.when(layer < other)
         def _():

time: 19.4 us -> 18.9 us (0.974)
  Pallas kernels: 18.6 us -> 17.9 us
    pallas_call x1, Pallas kernels: 17.8 us -> 17.2 us  [on_device(): pl.pallas_call(functools.partial(block_kernel, n, len(loaded)), out_shape...]
where the time goes in v5:
time: 18.9 us; the launch traced here: 18.6 us
  Pallas kernels  17.9 us (95%)
  between operations  0.65 us (3%)
    pallas_call x1, Pallas kernels, on_device(): pl.pallas_call(functools.partial(block_kernel, n, len(loaded)), out_shape...  17.2 us
    pallas_call x1, Pallas kernels, on_device(): pl.pallas_call(put_out, out_shape=(jax.ShapeDtypeStruct(edge_out.shape, b...  0.72 us

profile of v5, /device:TPU:29, one launch (start us, length us, event | category | flops | bytes accessed | tf_op | source)
XLA Modules:
  0.0 18.6 jit_solution(13441194801265392909)
XLA Ops:
  0.6 17.2 %block.1 = (bf16[256,512]{1,0:T(8,128)(2,1)S(1)}, bf16[16,256]{1,0:T(8,128)(2,1)S(1)}) custom-call(bf16[16,256]{1,0:T(8,128)(2,1)} %refs_0_.1, s32[1,128]{1,0:T(1,128)} %bitcast.17, bf16[256,512]{1,0:T(8,128)(2,1)} %refs_2_.1, bf16[512,512]{1,0:T(8,128)(2,1)} %refs_3_.1, s32[1,256]{1,0:T(1,128)} %bitcast.15, bf16[256,512]{1,0:T(8,128)(2,1)} %refs_5_.1, ...), custom_call_target="tpu_custom_call" | custom-call | tf_op jit(solution)/shard_map/block/pallas_call | solution.py:532
  17.9 0.7 %tail.1 = (bf16[256,512]{1,0:T(8,128)(2,1)}, bf16[16,256]{1,0:T(8,128)(2,1)}) custom-call(bf16[256,512]{1,0:T(8,128)(2,1)S(1)} %get-tuple-element.4.edge_v, bf16[16,256]{1,0:T(8,128)(2,1)S(1)} %get-tuple-element.5.atom_v), custom_call_target="tpu_custom_call" | custom-call | tf_op jit(solution)/shard_map/tail/pallas_call | solution.py:573

commit v6 on v5

--- a/solution.py
+++ b/solution.py
@@ -240,6 +240,7 @@
         rows_odd,
         hots_even,
         hots_odd,
+        edges_v,
         chain_v,
         sum_v,
         load_sem,
@@ -356,21 +357,18 @@
     for stage in stages:
         stage.wait()
     ends_out[...] = stage_v[...].astype(jnp.int16)
-    for tile in range(n):
-        basis_out[tile] = stage_basis_v[:, tile * cap : (tile + 1) * cap] * valid_v[tile].astype(
-            jnp.float32
-        ).astype(bf16)
-    own(0)
-    own(1)
     for other in range(layers):
+        for tile in range(other * span, (other + 1) * span):
+            basis_out[tile] = stage_basis_v[:, tile * cap : (tile + 1) * cap] * valid_v[
+                tile
+            ].astype(jnp.float32).astype(bf16)
 
         @pl.when(layer == other)
         def _():
-            send((0, 1), other)
-
-    for other in range(layers):
-
-        @pl.when(layer > other)
+            own(0)
+            own(1)
+
+        @pl.when(layer >= other)
         def _():
             send((0, 1), other)
 
@@ -384,6 +382,17 @@
     pick = hot_columns(atoms_in.shape[0] * atoms_in.shape[1], source_v[...])
     for load in loads[8:]:
         load.wait()
+    def first_of(apart):
+        return partner(layer, apart, layers) * span
+
+    def find(apart):
+        for i in range(span):
+            tile = first_of(apart) + i
+            ends = ends_v[tile].astype(jnp.int32) & (cap - 1)
+            edges_v[apart % 2, i] = look_up(send_v[tile], ends[:rows])
+            targets = look_up(return_v[tile], ends[rows:])
+            hots_v[apart % 2][i] = hot_from(edge_count, targets)
+
     for other in range(1, layers):
 
         @pl.when(layer < other)
@@ -397,9 +406,10 @@
         def _():
             send((0, 1), other)
 
-    arrive(atoms_in, recv_sem.at[2, 0])
     for kind, buffer in enumerate(arrays[:2]):
         arrive(buffer.at[pl.ds(layer * span, span)], recv_sem.at[kind, 0])
+    find(0)
+    arrive(atoms_in, recv_sem.at[2, 0])
     arrived = atoms_in[...].astype(jnp.float32).reshape(pick.shape[0], -1).astype(bf16)
     src_rows = dot_at(pick, arrived, 0, 0).astype(bf16)
     activated = silu(pre_act + matmul(src_rows, w_source_v[...])).astype(bf16)
@@ -410,17 +420,13 @@
     inner_two = silu(matmul(middle, w_res_v[2])).astype(bf16)
     chain_v[...] = (middle.astype(jnp.float32) + silu(matmul(inner_two, w_res_v[3]))) * inv_root
 
-    def first_of(apart):
-        return partner(layer, apart, layers) * span
-
     def prepare(apart):
+        if apart:
+            find(apart)
         for i in range(span):
-            tile = first_of(apart) + i
-            ends = ends_v[tile].astype(jnp.int32) & (cap - 1)
-            edges = look_up(send_v[tile], ends[:rows])
-            rows_v[apart % 2][i] = pick_columns(projected.astype(jnp.float32), edges).astype(bf16)
-            targets = look_up(return_v[tile], ends[rows:])
-            hots_v[apart % 2][i] = hot_from(edge_count, targets)
+            rows_v[apart % 2][i] = pick_columns(
+                projected.astype(jnp.float32), edges_v[apart % 2, i]
+            ).astype(bf16)
 
     def add_terms(apart):
         share = basis_count // HALVES
@@ -553,6 +559,7 @@
             pltpu.VMEM((n // layers, width, cap), bf16),
             pltpu.VMEM((n // layers, edge_count, cap), bf16),
             pltpu.VMEM((n // layers, edge_count, cap), bf16),
+            pltpu.VMEM((2, n // layers, 8, cap), jnp.int32),
             pltpu.VMEM((edge_count, edge_width), jnp.float32),
             pltpu.VMEM((basis_count * width, edge_count), jnp.float32),
             pltpu.SemaphoreType.DMA((len(loaded),)),

time: 18.9 us -> 18.9 us (level)
  no operation moved by 1% of the time
where the time goes in v6:
time: 18.9 us; the launch traced here: 18.5 us
  Pallas kernels  17.9 us (95%)
  between operations  0.65 us (3%)
    pallas_call x1, Pallas kernels, on_device(): pl.pallas_call(functools.partial(block_kernel, n, len(loaded)), out_shape...  17.2 us
    pallas_call x1, Pallas kernels, on_device(): pl.pallas_call(put_out, out_shape=(jax.ShapeDtypeStruct(edge_out.shape, b...  0.72 us

profile of v6, /device:TPU:29, one launch (start us, length us, event | category | flops | bytes accessed | tf_op | source)
XLA Modules:
  0.0 18.5 jit_solution(12686843865427775511)
XLA Ops:
  0.6 17.2 %block.1 = (bf16[256,512]{1,0:T(8,128)(2,1)S(1)}, bf16[16,256]{1,0:T(8,128)(2,1)S(1)}) custom-call(bf16[16,256]{1,0:T(8,128)(2,1)} %refs_0_.1, s32[1,128]{1,0:T(1,128)} %bitcast.17, bf16[256,512]{1,0:T(8,128)(2,1)} %refs_2_.1, bf16[512,512]{1,0:T(8,128)(2,1)} %refs_3_.1, s32[1,256]{1,0:T(1,128)} %bitcast.15, bf16[256,512]{1,0:T(8,128)(2,1)} %refs_5_.1, ...), custom_call_target="tpu_custom_call" | custom-call | tf_op jit(solution)/shard_map/block/pallas_call | solution.py:538
  17.8 0.7 %tail.1 = (bf16[256,512]{1,0:T(8,128)(2,1)}, bf16[16,256]{1,0:T(8,128)(2,1)}) custom-call(bf16[256,512]{1,0:T(8,128)(2,1)S(1)} %get-tuple-element.4.edge_v, bf16[16,256]{1,0:T(8,128)(2,1)S(1)} %get-tuple-element.5.atom_v), custom_call_target="tpu_custom_call" | custom-call | tf_op jit(solution)/shard_map/tail/pallas_call | solution.py:580
